TPU v7x, 32 devices: a whole 2x2x4 slice. The times are simulated.
32 devices in a mesh: dp: 2 (over x), tp: 4 (over z), section: 4 (over y, core).
Axes of the slice: x: 2, y: 2, z: 4, core: 2. Of those that a mesh axis runs over, the one named last changes fastest.
Arguments:
- tokens: bfloat16 [256, 2304], P('dp', 'section'), may hold values from -6 to 6
- hidden_grad: bfloat16 [256, 18432], P('dp', ('tp', 'section')), may hold values from -6 to 6
- norm_gain: float32 [2304], replicated, may hold values from 0.5 to 1.5
- w_gate: bfloat16 [2304, 18432], P('dp', ('tp', 'section')), may hold values from -0.125 to 0.125
- w_up: bfloat16 [2304, 18432], P('dp', ('tp', 'section')), may hold values from -0.125 to 0.125
Outputs:
- grad_tokens: bfloat16 [256, 2304], P('dp', ('tp', 'section'))
- grad_gain: float32 [2304], P(('tp', 'section'))
- grad_gate: bfloat16 [2304, 18432], P('dp', ('tp', 'section'))
- grad_up: bfloat16 [2304, 18432], P('dp', ('tp', 'section'))
All inputs are finite; a program needn't handle non-finite values.
Results may differ from a plain program's by a relative error of at most 0.018.
Values may be sent and summed in bfloat16 or wider, within the bound.
A program may use at most 128 MiB of HBM per device.

v0:
```python
import jax
import jax.numpy as jnp
from jax import lax
from jax.sharding import PartitionSpec as P

D = 2304
epsilon = 1e-06


def gated_unit(gate, up):
    return jax.nn.gelu(gate, approximate=True) * up


def shards(tokens, hidden_grad, norm_gain, w_gate, w_up):
    rows_in = lax.all_gather(tokens, "section", axis=1, tiled=True)
    inputs = rows_in.astype(jnp.float32)
    inv_rms = lax.rsqrt(jnp.mean(inputs * inputs, axis=1) + epsilon)
    normed = (inputs * inv_rms[:, None] * norm_gain).astype(jnp.bfloat16)
    full_gate, full_up = (
        lax.all_gather(w_gate, "dp", axis=0, tiled=True),
        lax.all_gather(w_up, "dp", axis=0, tiled=True),
    )
    gate = jnp.dot(normed, full_gate, preferred_element_type=jnp.float32)
    up = jnp.dot(normed, full_up, preferred_element_type=jnp.float32)
    hidden, pull = jax.vjp(gated_unit, gate, up)
    d_gate, d_up = pull(hidden_grad.astype(jnp.float32))
    d_gate = d_gate.astype(jnp.bfloat16)
    d_up = d_up.astype(jnp.bfloat16)
    contract_cols = (((1,), (1,)), ((), ()))
    contract_rows = (((0,), (0,)), ((), ()))
    features = full_gate.shape[0]
    own_width = features // lax.axis_size(("tp", "section"))
    first = lax.dot_general(full_gate, d_gate, contract_cols, preferred_element_type=jnp.float32)
    second = lax.dot_general(full_up, d_up, contract_cols, preferred_element_type=jnp.float32)
    d_columns = lax.psum_scatter(
        (first + second).astype(jnp.bfloat16), ("tp", "section"), scatter_dimension=0, tiled=True
    ).astype(jnp.float32)
    d_normed = d_columns.T
    offset = lax.axis_index(("tp", "section")) * own_width
    own_inputs = lax.dynamic_slice_in_dim(inputs, offset, own_width, 1)
    own_gain = lax.dynamic_slice_in_dim(norm_gain, offset, own_width, 0)
    gain_part = jnp.sum(d_normed * own_inputs * inv_rms[:, None], axis=0)
    row_part = jnp.sum(own_inputs * own_gain * d_normed, axis=1)
    grad_gain = lax.psum(gain_part, "dp")
    row_sum = lax.psum(row_part, ("tp", "section"))
    grad_tokens = (
        inv_rms[:, None] * own_gain * d_normed - own_inputs * (inv_rms**3 * row_sum / D)[:, None]
    )
    block = w_gate.shape[0]
    fwidth = w_gate.shape[1]
    cols_normed = lax.all_to_all(normed, "dp", split_axis=1, concat_axis=0, tiled=True)
    per_device = normed.shape[0]
    empty = jnp.zeros((block, fwidth), jnp.float32)
    piece_gate = lax.all_gather(d_gate, "dp", axis=0, tiled=True)
    piece_up = lax.all_gather(d_up, "dp", axis=0, tiled=True)

    def one_block(index, running):
        inner = index * per_device
        block_normed = lax.dynamic_slice_in_dim(cols_normed, inner, per_device, 0)
        block_gate = lax.dynamic_slice_in_dim(piece_gate, inner, per_device, 0)
        block_up = lax.dynamic_slice_in_dim(piece_up, inner, per_device, 0)
        terms = (
            lax.dot_general(
                block_normed, block_gate, contract_rows, preferred_element_type=jnp.float32
            ),
            lax.dot_general(
                block_normed, block_up, contract_rows, preferred_element_type=jnp.float32
            ),
        )
        return tuple(
            (
                total + lax.optimization_barrier(term.astype(jnp.bfloat16)).astype(jnp.float32)
                for total, term in zip(running, terms)
            )
        )

    sum_gate, sum_up = lax.fori_loop(
        0, piece_gate.shape[0] // per_device, one_block, (empty, empty)
    )
    return (
        grad_tokens.astype(jnp.bfloat16),
        grad_gain,
        sum_gate.astype(jnp.bfloat16),
        sum_up.astype(jnp.bfloat16),
    )


def solution(mesh):
    in_specs = (
        P("dp", "section"),
        P("dp", ("tp", "section")),
        P(),
        P("dp", ("tp", "section")),
        P("dp", ("tp", "section")),
    )
    out_specs = (
        P("dp", ("tp", "section")),
        P(("tp", "section")),
        P("dp", ("tp", "section")),
        P("dp", ("tp", "section")),
    )
    return jax.shard_map(shards, mesh=mesh, in_specs=in_specs, out_specs=out_specs, check_vma=False)
```

profile of v0, /device:TPU:0, one launch (start us, length us, event | category | flops | bytes accessed | tf_op | source)
XLA Modules:
  0.0 266.3 jit_solution(6498756828406113752)
XLA Ops:
  7.2 0.0 copy-start.3
  7.2 0.0 copy-start.4
  7.2 0.0 all-gather.5.cloned.1.call-start
  7.2 0.7 all-gather.5.cloned.1.call-update
  7.9 0.0 copy-start.2
  7.9 0.0 all-gather.3.cloned.1.call-start
  8.0 0.7 all-gather.3.cloned.1.call-update
  8.7 0.0 copy-done.3
  8.7 9.0 %all_gather.15 = bf16[128,2304]{0,1:T(8,128)(2,1)S(1)} all-gather(bf16[128,576]{0,1:T(8,128)(2,1)S(1)} %copy-done.3), channel_id=1, replica_groups=mesh['dp'=2,'tp'=4,'section'=4] {'section'}, dimensions={1}, use_global_device_ids=true | all-gather | bytes 737280 | tf_op jit(solution)/shard_map/all_gather | solution.py:15
  17.7 0.3 multiply_reduce_fusion
  18.1 0.0 copy-done.4
  18.1 0.4 multiply_convert_fusion
  18.4 1.1 copy.13
  19.5 3.5 %all-to-all-start = ((bf16[128,2,1152]{2,0,1:T(8,128)(2,1)}), bf16[128,2,1152]{2,0,1:T(8,128)(2,1)S(1)}, u32[]{:S(2)}, u32[]{:S(2)}) async-start(bf16[128,2,1152]{2,0,1:T(8,128)(2,1)} %copy.13), calls=%async_computation | async-start | bytes 1179648 | tf_op jit(solution)/shard_map/all_to_all | solution.py:51
  23.0 0.0 reduce-scatter.4.cloned.1.call-start
  23.1 1.1 convert_element_type.59
  24.2 0.1 dynamic_slice.27
  24.3 63.6 %all-gather.5.cloned.1.call-done = bf16[2304,1152]{1,0:T(8,128)(2,1)} async-done(((bf16[1152,1152]{1,0:T(8,128)(2,1)}), bf16[2304,1152]{1,0:T(8,128)(2,1)}) %all-gather.5.cloned.1.call-update) | async-done | bytes 5308432 | tf_op jit(solution)/shard_map/all_gather | solution.py:20
  87.9 0.0 copy-done.2
  87.9 3.7 %fusion.8 = (bf16[128,1152]{1,0:T(8,128)(2,1)S(1)}, f32[128,1152]{1,0:T(8,128)S(1)}) fusion(bf16[128,1152]{1,0:T(8,128)(2,1)S(1)} %copy-done.2, bf16[128,2304]{0,1:T(8,128)(2,1)S(1)} %multiply_convert_fusion, bf16[2304,1152]{1,0:T(8,128)(2,1)} %all-gather.5.cloned.1.call-done), kind=kOutput, calls=%fused_computation.19 | convolution fusion | flops 681099264 | bytes 7077888 | tf_op jit(solution)/shard_map/dot_general | solution.py:23
  91.6 67.1 %all-gather.3.cloned.1.call-done = bf16[2304,1152]{1,0:T(8,128)(2,1)} async-done(((bf16[1152,1152]{1,0:T(8,128)(2,1)}), bf16[2304,1152]{1,0:T(8,128)(2,1)}) %all-gather.3.cloned.1.call-update) | async-done | bytes 5308432 | tf_op jit(solution)/shard_map/all_gather | solution.py:21
  158.7 4.0 %fusion.15 = bf16[128,1152]{1,0:T(8,128)(2,1)S(1)} fusion(f32[128,1152]{1,0:T(8,128)S(1)} %get-tuple-element.158, bf16[128,2304]{0,1:T(8,128)(2,1)S(1)} %multiply_convert_fusion, bf16[2304,1152]{1,0:T(8,128)(2,1)} %all-gather.3.cloned.1.call-done, bf16[128,1152]{1,0:T(8,128)(2,1)} %param.8), kind=kOutput, calls=%fused_computation.26 | convolution fusion | flops 682721280 | bytes 7077888 | tf_op jit(solution)/shard_map/dot_general | solution.py:24
  162.7 0.0 slice-done
  162.7 0.0 slice-done.1
  162.7 0.0 copy-start.1
  162.7 1.6 fusion.23
  164.3 0.9 copy-done.1
  165.2 1.6 fusion.7
  166.8 1.1 copy.14
  167.9 0.0 reduce-scatter.4.cloned.1.call-update
  167.9 9.3 %all_gather.19 = bf16[256,1152]{1,0:T(8,128)(2,1)} all-gather(bf16[128,1152]{1,0:T(8,128)(2,1)S(1)} %get-tuple-element.157), channel_id=1, replica_groups=mesh['dp'=2,'tp'=4,'section'=4] {'dp'}, dimensions={0}, use_global_device_ids=true | all-gather | bytes 884736 | tf_op jit(solution)/shard_map/all_gather | solution.py:55
  177.2 8.5 %all_gather.18 = bf16[256,1152]{1,0:T(8,128)(2,1)} all-gather(bf16[128,1152]{1,0:T(8,128)(2,1)S(1)} %fusion.15), channel_id=1, replica_groups=mesh['dp'=2,'tp'=4,'section'=4] {'dp'}, dimensions={0}, use_global_device_ids=true | all-gather | bytes 884736 | tf_op jit(solution)/shard_map/all_gather | solution.py:54
  185.7 0.0 all-to-all-done
  185.7 27.0 %while.16 = (s32[]{:T(128)}, f32[1152,1152]{1,0:T(8,128)}, f32[1152,1152]{1,0:T(8,128)}, bf16[256,1152]{1,0:T(8,128)(2,1)S(1)}, bf16[256,1152]{1,0:T(8,128)(2,1)...) while((s32[]{:T(128)}, f32[1152,1152]{1,0:T(8,128)}, ...), condition=%wide.region_7.0_spmd.clone, body=%wide.region_6.0_spmd.clone.sunk | while | flops 690094080 | bytes 33032356 | solution.py:77
  185.7 1.8 convolution_convert_fusion.4
  187.6 3.4 %convolution_convert_fusion.5 = bf16[1152,1152]{1,0:T(8,128)(2,1)} fusion(bf16[256,1152]{1,0:T(8,128)(2,1)} %get-tuple-element.224, s32[]{:T(128)S(6)} %select_n.16, bf16[256,1152]{1,0:T(8,128)(2,1)S(1)} %get-tuple-element.223), kind=kOutput, calls=%fused_computation.1.clone.1 | convolution fusion | flops 341065728 | bytes 3245056 | tf_op jit(solution)/shard_map/while/body/eval_jaxpr/dot_general | solution.py:63
  190.9 6.7 %select_add_fusion.3 = (f32[1152,1152]{1,0:T(8,128)}, f32[1152,1152]{1,0:T(8,128)}) fusion(f32[1152,1152]{1,0:T(8,128)} %get-tuple-element.212, bf16[1152,1152]{1,0:T(8,128)(2,1)S(1)} %convolution_convert_fusion.4, pred[]{:T(512)S(6)} %compare.3, bf16[1152,1152]{1,0:T(8,128)(2,1)} %convolution_convert_fusion.5, f32[1152,1152]{1,0:T(8,128)} %get-tuple-element.211), kind=kLoop, calls=%fused_computation.2.clone.1 | loop fusion | flops 7962624 | bytes 26542080 | tf_op jit(solution)/shard_map/while/body/eval_jaxpr/add | solution.py:72
  197.6 1.8 convolution_convert_fusion.4
  199.5 3.4 %convolution_convert_fusion.5 = bf16[1152,1152]{1,0:T(8,128)(2,1)} fusion(bf16[256,1152]{1,0:T(8,128)(2,1)} %get-tuple-element.224, s32[]{:T(128)S(6)} %select_n.16, bf16[256,1152]{1,0:T(8,128)(2,1)S(1)} %get-tuple-element.223), kind=kOutput, calls=%fused_computation.1.clone.1 | convolution fusion | flops 341065728 | bytes 3245056 | tf_op jit(solution)/shard_map/while/body/eval_jaxpr/dot_general | solution.py:63
  202.8 9.9 %select_add_fusion.3 = (f32[1152,1152]{1,0:T(8,128)}, f32[1152,1152]{1,0:T(8,128)}) fusion(f32[1152,1152]{1,0:T(8,128)} %get-tuple-element.212, bf16[1152,1152]{1,0:T(8,128)(2,1)S(1)} %convolution_convert_fusion.4, pred[]{:T(512)S(6)} %compare.3, bf16[1152,1152]{1,0:T(8,128)(2,1)} %convolution_convert_fusion.5, f32[1152,1152]{1,0:T(8,128)} %get-tuple-element.211), kind=kLoop, calls=%fused_computation.2.clone.1 | loop fusion | flops 7962624 | bytes 26542080 | tf_op jit(solution)/shard_map/while/body/eval_jaxpr/add | solution.py:72
  212.7 4.4 %convert_element_type.68 = bf16[1152,1152]{1,0:T(8,128)(2,1)} convert(f32[1152,1152]{1,0:T(8,128)} %get-tuple-element.115) | non-fusion elementwise | flops 1327104 | bytes 7962624 | tf_op jit(solution)/shard_map/convert_element_type | solution.py:84
  217.1 0.2 copy-done
  217.3 1.8 convert_element_type.67
  219.1 3.0 %reduce-scatter.4.cloned.1.call-done = bf16[144,128]{1,0:T(8,128)(2,1)} async-done(((bf16[2304,128]{1,0:T(8,128)(2,1)}), bf16[144,128]{1,0:T(8,128)(2,1)}) %reduce-scatter.4.cloned.1.call-update) | async-done | bytes 36880 | tf_op jit(solution)/shard_map/reduce_scatter | solution.py:35
  222.1 1.1 fusion.20
  223.2 5.5 %psum.15 = f32[144]{0:T(256)} all-reduce(f32[144]{0:T(256)S(1)} %get-tuple-element.141), channel_id=1, replica_groups=mesh['dp'=2,'tp'=4,'section'=4] {'dp'}, use_global_device_ids=true, to_apply=%region_5.0 | all-reduce | flops 144 | bytes 1152 | tf_op jit(solution)/shard_map/psum | solution.py:44
  228.6 29.5 %psum.14 = f32[128]{0:T(128)S(1)} all-reduce(f32[128]{0:T(128)S(1)} %get-tuple-element.142), channel_id=1, replica_groups=mesh['dp'=2,'tp'=4,'section'=4] {'tp','section'}, use_global_device_ids=true, to_apply=%region_3.0 | all-reduce | flops 128 | bytes 1024 | tf_op jit(solution)/shard_map/psum | solution.py:45
  258.1 1.6 fusion.17
  (8 shorter events, 0.0 us)
Async XLA Ops:
  7.2 1.5 copy-start.3
  7.2 10.9 %copy-start.4 = (f32[2304]{0:T(1024)S(1)}, f32[2304]{0:T(1024)}, u32[]{:S(2)}) copy-start(f32[2304]{0:T(1024)} %param.9) | copy-start | bytes 27652
  7.2 80.7 %all-gather.5.cloned.1.call-start = ((), (), s32[]{:S(2)}) async-start(), calls=%async_computation.3 | async-start | bytes 7962624 | tf_op jit(solution)/shard_map/all_gather | solution.py:20
  7.9 80.0 %copy-start.2 = (bf16[128,1152]{1,0:T(8,128)(2,1)S(1)}, bf16[128,1152]{1,0:T(8,128)(2,1)}, u32[]{:S(2)}) copy-start(bf16[128,1152]{1,0:T(8,128)(2,1)} %param.8) | copy-start | bytes 884740
  7.9 150.8 %all-gather.3.cloned.1.call-start = ((), (), s32[]{:S(2)}) async-start(), calls=%async_computation.2 | async-start | bytes 7962624 | tf_op jit(solution)/shard_map/all_gather | solution.py:21
  19.5 166.2 %all-to-all-start = ((bf16[128,2,1152]{2,0,1:T(8,128)(2,1)}), bf16[128,2,1152]{2,0,1:T(8,128)(2,1)S(1)}, u32[]{:S(2)}, u32[]{:S(2)}) async-start(bf16[128,2,1152]{2,0,1:T(8,128)(2,1)} %copy.13), calls=%async_computation | async-start | bytes 1179648 | tf_op jit(solution)/shard_map/all_to_all | solution.py:51
  23.0 199.1 %reduce-scatter.4.cloned.1.call-start = ((), (), s32[]{:S(2)}) async-start(), calls=%async_computation.4 | async-start | bytes 626688 | tf_op jit(solution)/shard_map/reduce_scatter | solution.py:35
  87.9 74.8 %slice-start = ((s8[5308416]{0:T(1024)(128)(4,1)}), s8[1114112]{0:T(1024)(128)(4,1)S(1)}, s32[]{:S(2)}) async-start(s8[5308416]{0:T(1024)(128)(4,1)} %bitcast.30), calls=%async_computation.5 | async-start | bytes 2228224
  158.7 4.0 %slice-start.1 = ((s8[5308416]{0:T(1024)(128)(4,1)}), s8[4194304]{0:T(1024)(128)(4,1)S(1)}, s32[]{:S(2)}) async-start(s8[5308416]{0:T(1024)(128)(4,1)} %bitcast.30), calls=%async_computation.6 | async-start | bytes 8388608
  162.7 2.5 copy-start.1
  212.7 4.7 %copy-start = (f32[1152,1152]{1,0:T(8,128)S(1)}, f32[1152,1152]{1,0:T(8,128)}, u32[]{:S(2)}) copy-start(f32[1152,1152]{1,0:T(8,128)} %get-tuple-element.114) | copy-start | bytes 15925252
Sparse Core Ops, SparseCore 0:
  9.5 78.3 all-gather.4
  89.4 69.2 all-gather.2
  168.0 54.0 reduce-scatter.3
where the time goes:
time: 267 us; the launch traced here: 266 us
  waiting for transfers between devices  135 us (51%)
  blocking collectives  61.8 us (23%)
  other arithmetic  27.3 us (10%)
  matrix products  21.2 us (8%)
  between operations  13.9 us (5%)
  starting transfers between devices  3.64 us (1%)
  local copies, waits for them, and re-layouts  3.38 us (1%)
    all_gather x1, waiting for transfers between devices, shards(): lax.all_gather(w_up, 'dp', axis=0, tiled=True)  67.1 us
    all_gather x1, waiting for transfers between devices, shards(): lax.all_gather(w_gate, 'dp', axis=0, tiled=True)  63.6 us
    psum x1, blocking collectives, shards(): row_sum = lax.psum(row_part, ('tp', 'section'))  29.5 us
    add x2, other arithmetic, one_block(): total + lax.optimization_barrier(term.astype(jnp.bfloat16)).astype(jnp.fl...  16.6 us
    all_gather x1, blocking collectives, shards(): piece_up = lax.all_gather(d_up, 'dp', axis=0, tiled=True)  9.34 us
    all_gather x1, blocking collectives, shards(): rows_in = lax.all_gather(tokens, 'section', axis=1, tiled=True)  9.03 us
    all_gather x1, blocking collectives, shards(): piece_gate = lax.all_gather(d_gate, 'dp', axis=0, tiled=True)  8.47 us
    dot_general x2, matrix products, one_block(): lax.dot_general(block_normed, block_gate, contract_rows, preferred_elemen...  6.71 us
  transfers between devices with their start and end apart: 4, of which 3 were waited for; matrix products, arithmetic and copies ran while one was open for 18% of the time, Pallas kernels for 0%

commit v1 on v0

--- a/solution.py
+++ b/solution.py
@@ -51,8 +51,11 @@
     cols_normed = lax.all_to_all(normed, "dp", split_axis=1, concat_axis=0, tiled=True)
     per_device = normed.shape[0]
     empty = jnp.zeros((block, fwidth), jnp.float32)
-    piece_gate = lax.all_gather(d_gate, "dp", axis=0, tiled=True)
-    piece_up = lax.all_gather(d_up, "dp", axis=0, tiled=True)
+    piece_gate, piece_up = jnp.split(
+        lax.all_gather(jnp.concatenate([d_gate, d_up], axis=1), "dp", axis=0, tiled=True),
+        [d_gate.shape[1]],
+        axis=1,
+    )
 
     def one_block(index, running):
         inner = index * per_device

time: 267 us -> 296 us (1.11)
  waiting for transfers between devices: 135 us -> 180 us
  blocking collectives: 61.8 us -> 44.1 us
    reduce_scatter x1, waiting for transfers between devices: 2.99 us -> 48.5 us  [shards(): lax.psum_scatter((first + second).astype(jnp.bfloat16), ('tp', 'section')...]
    all_gather x2 -> x0, blocking collectives: 17.8 us -> none  [the longest x1 9.34 us: shards(): piece_up = lax.all_gather(d_up, 'dp', axis=0, tiled=True)]
  transfers between devices with their start and end apart: 4 -> 5, of which waited for: 3 -> 3; matrix products, arithmetic and copies ran while one was open for 18% -> 4% of each run, Pallas kernels for 0% -> 0%
where the time goes in v1:
time: 296 us
  waiting for transfers between devices  180 us (61%)
  blocking collectives  44.1 us (15%)
  other arithmetic  26.9 us (9%)
  matrix products  21.2 us (7%)
  between operations  13.9 us (5%)
  local copies, waits for them, and re-layouts  5.68 us (2%)
  starting transfers between devices  3.66 us (1%)
    all_gather x1, waiting for transfers between devices, shards(): lax.all_gather(w_up, 'dp', axis=0, tiled=True)  67.1 us
    all_gather x1, waiting for transfers between devices, shards(): lax.all_gather(w_gate, 'dp', axis=0, tiled=True)  63.1 us
    reduce_scatter x1, waiting for transfers between devices, shards(): lax.psum_scatter((first + second).astype(jnp.bfloat16), ('tp', 'section')...  48.5 us
    psum x1, blocking collectives, shards(): row_sum = lax.psum(row_part, ('tp', 'section'))  29.6 us
    add x2, other arithmetic, one_block(): total + lax.optimization_barrier(term.astype(jnp.bfloat16)).astype(jnp.fl...  16.6 us
    all_gather x1, blocking collectives, shards(): rows_in = lax.all_gather(tokens, 'section', axis=1, tiled=True)  9.03 us
    dot_general x2, matrix products, one_block(): lax.dot_general(block_normed, block_gate, contract_rows, preferred_elemen...  6.71 us
  transfers between devices with their start and end apart: 5, of which 3 were waited for; matrix products, arithmetic and copies ran while one was open for 4% of the time, Pallas kernels for 0%

profile of v1, /device:TPU:0, one launch (start us, length us, event | category | flops | bytes accessed | tf_op | source)
XLA Modules:
  0.0 295.6 jit_solution(8659170785841820043)
XLA Ops:
  7.2 0.0 copy-start.3
  7.2 0.0 copy-start.4
  7.2 0.0 copy-start.2
  7.2 0.0 all-gather.6.cloned.1.call-start
  7.2 0.7 all-gather.6.cloned.1.call-update
  7.9 0.0 all-gather.4.cloned.1.call-start
  8.0 0.7 all-gather.4.cloned.1.call-update
  8.7 0.0 reduce-scatter.4.cloned.1.call-start
  8.7 0.0 copy-done.3
  8.7 9.0 %all_gather.12 = bf16[128,2304]{0,1:T(8,128)(2,1)S(1)} all-gather(bf16[128,576]{0,1:T(8,128)(2,1)S(1)} %copy-done.3), channel_id=1, replica_groups=mesh['dp'=2,'tp'=4,'section'=4] {'section'}, dimensions={1}, use_global_device_ids=true | all-gather | bytes 737280 | tf_op jit(solution)/shard_map/all_gather | solution.py:15
  17.8 0.3 multiply_reduce_fusion
  18.1 0.4 multiply_convert_fusion
  18.5 63.1 %all-gather.6.cloned.1.call-done = bf16[2304,1152]{1,0:T(8,128)(2,1)} async-done(((bf16[1152,1152]{1,0:T(8,128)(2,1)}), bf16[2304,1152]{1,0:T(8,128)(2,1)}) %all-gather.6.cloned.1.call-update) | async-done | bytes 5308432 | tf_op jit(solution)/shard_map/all_gather | solution.py:20
  81.6 3.7 %fusion.8 = (bf16[128,1152]{1,0:T(8,128)(2,1)S(1)}, f32[128,1152]{1,0:T(8,128)S(1)}) fusion(bf16[128,1152]{1,0:T(8,128)(2,1)S(1)} %copy-done.2, bf16[128,2304]{0,1:T(8,128)(2,1)S(1)} %multiply_convert_fusion, bf16[2304,1152]{1,0:T(8,128)(2,1)} %all-gather.6.cloned.1.call-done), kind=kOutput, calls=%fused_computation.19 | convolution fusion | flops 681099264 | bytes 7077888 | tf_op jit(solution)/shard_map/dot_general | solution.py:23
  85.3 67.1 %all-gather.4.cloned.1.call-done = bf16[2304,1152]{1,0:T(8,128)(2,1)} async-done(((bf16[1152,1152]{1,0:T(8,128)(2,1)}), bf16[2304,1152]{1,0:T(8,128)(2,1)}) %all-gather.4.cloned.1.call-update) | async-done | bytes 5308432 | tf_op jit(solution)/shard_map/all_gather | solution.py:21
  152.4 4.0 %fusion.15 = bf16[128,1152]{1,0:T(8,128)(2,1)S(1)} fusion(f32[128,1152]{1,0:T(8,128)S(1)} %get-tuple-element.160, bf16[128,2304]{0,1:T(8,128)(2,1)S(1)} %multiply_convert_fusion, bf16[2304,1152]{1,0:T(8,128)(2,1)} %all-gather.4.cloned.1.call-done, bf16[128,1152]{1,0:T(8,128)(2,1)} %param.8), kind=kOutput, calls=%fused_computation.26 | convolution fusion | flops 682721280 | bytes 7077888 | tf_op jit(solution)/shard_map/dot_general | solution.py:24
  156.4 0.0 slice-done
  156.4 0.0 slice-done.1
  156.4 0.0 copy-start.1
  156.4 1.6 fusion.24
  158.0 0.9 copy-done.1
  158.9 1.6 fusion.7
  160.5 1.1 copy.14
  161.6 0.0 reduce-scatter.4.cloned.1.call-update
  161.6 0.0 all-gather.8.cloned.1.call-start
  161.6 0.9 pad_maximum_fusion
  162.5 0.0 all-gather.8.cloned.1.call-update
  162.5 1.1 copy.13
  163.6 3.5 %all-to-all-start = ((bf16[128,2,1152]{2,0,1:T(8,128)(2,1)}), bf16[128,2,1152]{2,0,1:T(8,128)(2,1)S(1)}, u32[]{:S(2)}, u32[]{:S(2)}) async-start(bf16[128,2,1152]{2,0,1:T(8,128)(2,1)} %copy.13), calls=%async_computation | async-start | bytes 1179648 | tf_op jit(solution)/shard_map/all_to_all | solution.py:51
  167.1 0.1 convert_element_type.59
  167.2 0.1 dynamic_slice.27
  167.3 48.5 %reduce-scatter.4.cloned.1.call-done = bf16[144,128]{1,0:T(8,128)(2,1)} async-done(((bf16[2304,128]{1,0:T(8,128)(2,1)}), bf16[144,128]{1,0:T(8,128)(2,1)}) %reduce-scatter.4.cloned.1.call-update) | async-done | bytes 36880 | tf_op jit(solution)/shard_map/reduce_scatter | solution.py:35
  215.8 0.9 fusion.20
  216.7 29.6 %psum.14 = f32[128]{0:T(128)S(1)} all-reduce(f32[128]{0:T(128)S(1)} %get-tuple-element.142), channel_id=1, replica_groups=mesh['dp'=2,'tp'=4,'section'=4] {'tp','section'}, use_global_device_ids=true, to_apply=%region_3.0 | all-reduce | flops 128 | bytes 1024 | tf_op jit(solution)/shard_map/psum | solution.py:45
  246.4 5.5 %psum.15 = f32[144]{0:T(256)} all-reduce(f32[144]{0:T(256)S(1)} %get-tuple-element.141), channel_id=1, replica_groups=mesh['dp'=2,'tp'=4,'section'=4] {'dp'}, use_global_device_ids=true, to_apply=%region_5.0 | all-reduce | flops 144 | bytes 1152 | tf_op jit(solution)/shard_map/psum | solution.py:44
  251.8 1.5 fusion.17
  253.3 2.4 fusion.23
  255.7 0.0 all-to-all-done
  255.7 27.0 %while.16 = (s32[]{:T(128)}, f32[1152,1152]{1,0:T(8,128)}, f32[1152,1152]{1,0:T(8,128)}, bf16[256,1152]{1,0:T(8,128)(2,1)S(1)}, bf16[256,1152]{1,0:T(8,128)(2,1)...) while((s32[]{:T(128)}, f32[1152,1152]{1,0:T(8,128)}, ...), condition=%wide.region_7.0_spmd.clone, body=%wide.region_6.0_spmd.clone.sunk | while | flops 690094080 | bytes 33032356 | solution.py:80
  255.7 1.8 convolution_convert_fusion.4
  257.5 3.4 %convolution_convert_fusion.5 = bf16[1152,1152]{1,0:T(8,128)(2,1)} fusion(bf16[256,1152]{1,0:T(8,128)(2,1)} %get-tuple-element.226, s32[]{:T(128)S(6)} %select_n.16, bf16[256,1152]{1,0:T(8,128)(2,1)S(1)} %get-tuple-element.225), kind=kOutput, calls=%fused_computation.1.clone.1 | convolution fusion | flops 341065728 | bytes 3245056 | tf_op jit(solution)/shard_map/while/body/eval_jaxpr/dot_general | solution.py:66
  260.9 6.8 %select_add_fusion.3 = (f32[1152,1152]{1,0:T(8,128)}, f32[1152,1152]{1,0:T(8,128)}) fusion(f32[1152,1152]{1,0:T(8,128)} %get-tuple-element.214, bf16[1152,1152]{1,0:T(8,128)(2,1)S(1)} %convolution_convert_fusion.4, pred[]{:T(512)S(6)} %compare.3, bf16[1152,1152]{1,0:T(8,128)(2,1)} %convolution_convert_fusion.5, f32[1152,1152]{1,0:T(8,128)} %get-tuple-element.213), kind=kLoop, calls=%fused_computation.2.clone.1 | loop fusion | flops 7962624 | bytes 26542080 | tf_op jit(solution)/shard_map/while/body/eval_jaxpr/add | solution.py:75
  267.7 1.8 convolution_convert_fusion.4
  269.5 3.4 %convolution_convert_fusion.5 = bf16[1152,1152]{1,0:T(8,128)(2,1)} fusion(bf16[256,1152]{1,0:T(8,128)(2,1)} %get-tuple-element.226, s32[]{:T(128)S(6)} %select_n.16, bf16[256,1152]{1,0:T(8,128)(2,1)S(1)} %get-tuple-element.225), kind=kOutput, calls=%fused_computation.1.clone.1 | convolution fusion | flops 341065728 | bytes 3245056 | tf_op jit(solution)/shard_map/while/body/eval_jaxpr/dot_general | solution.py:66
  272.9 9.9 %select_add_fusion.3 = (f32[1152,1152]{1,0:T(8,128)}, f32[1152,1152]{1,0:T(8,128)}) fusion(f32[1152,1152]{1,0:T(8,128)} %get-tuple-element.214, bf16[1152,1152]{1,0:T(8,128)(2,1)S(1)} %convolution_convert_fusion.4, pred[]{:T(512)S(6)} %compare.3, bf16[1152,1152]{1,0:T(8,128)(2,1)} %convolution_convert_fusion.5, f32[1152,1152]{1,0:T(8,128)} %get-tuple-element.213), kind=kLoop, calls=%fused_computation.2.clone.1 | loop fusion | flops 7962624 | bytes 26542080 | tf_op jit(solution)/shard_map/while/body/eval_jaxpr/add | solution.py:75
  282.7 4.4 %convert_element_type.68 = bf16[1152,1152]{1,0:T(8,128)(2,1)} convert(f32[1152,1152]{1,0:T(8,128)} %get-tuple-element.115) | non-fusion elementwise | flops 1327104 | bytes 7962624 | tf_op jit(solution)/shard_map/convert_element_type | solution.py:87
  287.2 0.1 copy-done
  287.3 1.8 convert_element_type.67
  (11 shorter events, 0.0 us)
Async XLA Ops:
  7.2 1.6 copy-start.3
  7.2 10.9 %copy-start.4 = (f32[2304]{0:T(1024)S(1)}, f32[2304]{0:T(1024)}, u32[]{:S(2)}) copy-start(f32[2304]{0:T(1024)} %param.9) | copy-start | bytes 27652
  7.2 74.4 %copy-start.2 = (bf16[128,1152]{1,0:T(8,128)(2,1)S(1)}, bf16[128,1152]{1,0:T(8,128)(2,1)}, u32[]{:S(2)}) copy-start(bf16[128,1152]{1,0:T(8,128)(2,1)} %param.8) | copy-start | bytes 884740
  7.2 74.4 %all-gather.6.cloned.1.call-start = ((), (), s32[]{:S(2)}) async-start(), calls=%async_computation.3 | async-start | bytes 7962624 | tf_op jit(solution)/shard_map/all_gather | solution.py:20
  7.9 144.5 %all-gather.4.cloned.1.call-start = ((), (), s32[]{:S(2)}) async-start(), calls=%async_computation.2 | async-start | bytes 7962624 | tf_op jit(solution)/shard_map/all_gather | solution.py:21
  8.7 207.2 %reduce-scatter.4.cloned.1.call-start = ((), (), s32[]{:S(2)}) async-start(), calls=%async_computation.5 | async-start | bytes 626688 | tf_op jit(solution)/shard_map/reduce_scatter | solution.py:35
  81.6 74.8 %slice-start = ((s8[5308416]{0:T(1024)(128)(4,1)}), s8[1114112]{0:T(1024)(128)(4,1)S(1)}, s32[]{:S(2)}) async-start(s8[5308416]{0:T(1024)(128)(4,1)} %bitcast.30), calls=%async_computation.6 | async-start | bytes 2228224
  152.4 4.0 %slice-start.1 = ((s8[5308416]{0:T(1024)(128)(4,1)}), s8[4194304]{0:T(1024)(128)(4,1)S(1)}, s32[]{:S(2)}) async-start(s8[5308416]{0:T(1024)(128)(4,1)} %bitcast.30), calls=%async_computation.7 | async-start | bytes 8388608
  156.4 2.5 copy-start.1
  161.6 91.7 %all-gather.8.cloned.1.call-start = ((), (), s32[]{:S(2)}) async-start(), calls=%async_computation.4 | async-start | bytes 1769472 | tf_op jit(solution)/shard_map/all_gather | solution.py:55
  163.6 92.1 %all-to-all-start = ((bf16[128,2,1152]{2,0,1:T(8,128)(2,1)}), bf16[128,2,1152]{2,0,1:T(8,128)(2,1)S(1)}, u32[]{:S(2)}, u32[]{:S(2)}) async-start(bf16[128,2,1152]{2,0,1:T(8,128)(2,1)} %copy.13), calls=%async_computation | async-start | bytes 1179648 | tf_op jit(solution)/shard_map/all_to_all | solution.py:51
  282.7 4.6 %copy-start = (f32[1152,1152]{1,0:T(8,128)S(1)}, f32[1152,1152]{1,0:T(8,128)}, u32[]{:S(2)}) copy-start(f32[1152,1152]{1,0:T(8,128)} %get-tuple-element.114) | copy-start | bytes 15925252
Sparse Core Ops, SparseCore 0:
  9.5 71.9 all-gather.5
  83.1 69.2 all-gather.3
  161.7 54.0 reduce-scatter.3
  217.2 21.7 all-gather.7
